TPU v7x, 32 devices: a whole 2x2x4 slice. The times are simulated.
32 devices in a mesh: dp: 8 (over y, x, core), mp: 4 (over z).
Axes of the slice: x: 2, y: 2, z: 4, core: 2. Of those that a mesh axis runs over, the one named last changes fastest.
Arguments:
- inputs: bfloat16 [1024, 6144], P('dp'), may hold values from -6 to 6
- pre_act: bfloat16 [1024, 12288], P('dp', 'mp'), may hold values from -6 to 6
- out_grad: bfloat16 [1024, 6144], P('dp'), may hold values from -6 to 6
- w_in: bfloat16 [6144, 12288], P(None, 'mp'), may hold values from -0.109375 to 0.109375
- w_out: bfloat16 [12288, 6144], P('mp'), may hold values from -0.0546875 to 0.0546875
- master_in: float32 [6144, 12288], P('dp', 'mp'), may hold values from -0.3 to 0.3
- master_out: float32 [12288, 6144], P('mp', 'dp'), may hold values from -0.3 to 0.3
- row_in: float32 [6144], P('dp'), may hold values from 12.8 to 686.08
- col_in: float32 [12288], P('mp'), may hold values from 25 to 128
- row_out: float32 [12288], P('mp'), may hold values from 25.6 to 1372.16
- col_out: float32 [6144], P('dp'), may hold values from 51 to 256
Outputs:
- input_grad: bfloat16 [1024, 6144], P('dp', 'mp')
- new_master_in: float32 [6144, 12288], P('dp', 'mp')
- new_master_out: float32 [12288, 6144], P('mp', 'dp')
All inputs are finite; a program needn't handle non-finite values.
Results may differ from a plain program's by a relative error of at most 0.012.
Values may be sent and summed in bfloat16 or wider, within the bound.
A program may use at most 256 MiB of HBM per device.

v0:
```python
import math
import jax
import jax.numpy as jnp
from jax import lax
from jax.sharding import PartitionSpec as P

D = 6144
FF = 12288
decay_rate = 0.8
step_size = 0.05
tiny_square = 1e-30


def gelu_parts(pre):
    cumulative = 0.5 * (1.0 + jax.scipy.special.erf(pre * (1.0 / math.sqrt(2.0))))
    density = jnp.exp(-0.5 * pre * pre) * (1.0 / math.sqrt(2.0 * math.pi))
    return (pre * cumulative, cumulative + pre * density)


def contract_rows(left, right):
    return lax.dot_general(
        left, right, (((0,), (0,)), ((), ())), preferred_element_type=jnp.float32
    )


def scatter_sum(partial, axis):
    size = lax.axis_size(axis)
    me = lax.axis_index(axis)
    width = partial.shape[1] // size
    piece = lambda k: lax.dynamic_slice_in_dim(partial, k * width, width, 1)
    total = piece(me)
    for shift in range(1, size):
        moved = piece(lax.rem(me + shift, size)).astype(jnp.bfloat16)
        got = lax.ppermute(moved, axis, [(i, (i + shift) % size) for i in range(size)])
        total = total + got.astype(jnp.float32)
    return total


def body(
    inputs, pre_act, out_grad, w_in, w_out, master_in, master_out, row_in, col_in, row_out, col_out
):
    active, slope = gelu_parts(pre_act.astype(jnp.float32))
    hidden_all = lax.all_gather(active.astype(jnp.bfloat16), "dp", axis=0, tiled=True)
    out_cols = lax.all_to_all(out_grad, "dp", 1, 0, tiled=True)
    in_cols = lax.all_to_all(inputs, "dp", 1, 0, tiled=True)
    hid_grad = lax.dot_general(
        out_grad, w_out, (((1,), (1,)), ((), ())), preferred_element_type=jnp.float32
    )
    pre_grad = (hid_grad * slope).astype(jnp.bfloat16)
    pre_grad_all = lax.all_gather(pre_grad, "dp", axis=0, tiled=True)
    input_part = lax.dot_general(
        pre_grad, w_in, (((1,), (1,)), ((), ())), preferred_element_type=jnp.float32
    )
    input_grad = scatter_sum(input_part, "mp").astype(jnp.bfloat16)
    grad_out = contract_rows(hidden_all, out_cols)
    grad_in = contract_rows(in_cols, pre_grad_all)
    square_in = grad_in * grad_in + tiny_square
    square_out = grad_out * grad_out + tiny_square
    width_in, width_out, row_out_sum = lax.psum(
        (jnp.sum(square_in, axis=1), jnp.sum(square_out, axis=0), jnp.sum(row_out)), "mp"
    )
    rows_in = decay_rate * row_in + (1.0 - decay_rate) * width_in / FF
    cols_out = decay_rate * col_out + (1.0 - decay_rate) * width_out / FF
    hidden_in, hidden_out, sum_in, sum_out = lax.psum(
        (
            jnp.sum(square_in, axis=0),
            jnp.sum(square_out, axis=1),
            jnp.sum(rows_in),
            jnp.sum(width_out),
        ),
        "dp",
    )
    cols_in = decay_rate * col_in + (1.0 - decay_rate) * hidden_in / D
    rows_out = decay_rate * row_out + (1.0 - decay_rate) * hidden_out / D
    mean_in = sum_in / D
    mean_out = (decay_rate * row_out_sum + (1.0 - decay_rate) * sum_out / D) / FF
    update_in = grad_in / jnp.sqrt(rows_in[:, None] * cols_in[None, :] / mean_in)
    update_out = grad_out / jnp.sqrt(rows_out[:, None] * cols_out[None, :] / mean_out)
    new_master_in = master_in - step_size * update_in
    new_master_out = master_out - step_size * update_out
    return (input_grad, new_master_in, new_master_out)


def solution(mesh):
    in_specs = (
        P("dp", None),
        P("dp", "mp"),
        P("dp", None),
        P(None, "mp"),
        P("mp", None),
        P("dp", "mp"),
        P("mp", "dp"),
        P("dp"),
        P("mp"),
        P("mp"),
        P("dp"),
    )
    out_specs = (P("dp", "mp"), P("dp", "mp"), P("mp", "dp"))
    return jax.shard_map(body, mesh=mesh, in_specs=in_specs, out_specs=out_specs, check_vma=False)
```

profile of v0, /device:TPU:0, one launch (start us, length us, event | category | flops | bytes accessed | tf_op | source)
XLA Modules:
  0.0 242.8 jit_solution(6734764929299141886)
XLA Ops:
  7.2 0.0 copy-start.1
  7.2 0.0 all-gather.3.cloned.1.call-start
  7.2 19.2 %fusion.7 = bf16[128,3072]{1,0:T(8,128)(2,1)} fusion(bf16[128,6144]{1,0:T(8,128)(2,1)} %param.13, bf16[3072,6144]{1,0:T(8,128)(2,1)} %param.15, bf16[128,3072]{1,0:T(8,128)(2,1)} %param.12), kind=kOutput, calls=%fused_computation.12 | convolution fusion | flops 4836163584 | bytes 40894464 | tf_op jit(solution)/shard_map/dot_general | solution.py:46
  26.4 0.0 copy-start.2
  26.4 0.0 all-gather.3.cloned.1.call-update
  26.5 0.0 all-gather.5.cloned.1.call-start
  26.5 2.5 %fusion.14 = bf16[128,3072]{1,0:T(8,128)(2,1)} fusion(bf16[128,3072]{1,0:T(8,128)(2,1)} %param.12), kind=kLoop, calls=%fused_computation.24 | loop fusion | flops 2359296 | bytes 1572864 | tf_op jit(solution)/shard_map/convert_element_type | solution.py:43
  29.0 0.0 all-gather.5.cloned.1.call-update
  29.0 0.0 copy-done.1
  29.0 1.6 copy.18
  30.6 5.2 %all-to-all-start = ((bf16[128,8,768]{0,2,1:T(8,128)(2,1)}), bf16[128,8,768]{0,2,1:T(8,128)(2,1)S(1)}, u32[]{:S(2)}, u32[]{:S(2)}) async-start(bf16[128,8,768]{0,2,1:T(8,128)(2,1)} %bitcast), calls=%async_computation | async-start | bytes 3145728 | tf_op jit(solution)/shard_map/all_to_all | solution.py:45
  35.8 0.0 copy-done.2
  35.8 1.7 copy.21
  37.5 27.7 %all-to-all-done = bf16[128,8,768]{0,2,1:T(8,128)(2,1)S(1)} async-done(((bf16[128,8,768]{0,2,1:T(8,128)(2,1)}), bf16[128,8,768]{0,2,1:T(8,128)(2,1)S(1)}, u32[]{:S(2)}, u32[]{:S(2)}) %all-to-all-start) | async-done | bytes 1572896 | tf_op jit(solution)/shard_map/all_to_all | solution.py:45
  65.2 0.0 copy-start
  65.2 1.1 copy-done
  66.3 4.3 %all-to-all-start.1 = ((bf16[128,8,768]{0,2,1:T(8,128)(2,1)}), bf16[128,8,768]{0,2,1:T(8,128)(2,1)}, u32[]{:S(2)}, u32[]{:S(2)}) async-start(bf16[128,8,768]{0,2,1:T(8,128)(2,1)} %bitcast.4), calls=%async_computation.1 | async-start | bytes 3145728 | tf_op jit(solution)/shard_map/all_to_all | solution.py:44
  70.6 18.0 %fusion.16 = f32[128,6144]{1,0:T(8,128)S(1)} fusion(bf16[128,3072]{1,0:T(8,128)(2,1)} %fusion.7, bf16[6144,3072]{1,0:T(8,128)(2,1)} %param.14), kind=kOutput, calls=%fused_computation.34 | convolution fusion | flops 4831838208 | bytes 41680896 | tf_op jit(solution)/shard_map/dot_general | solution.py:51
  88.6 1.0 dynamic-slice_convert_fusion.2
  89.6 1.6 collective-permute-start
  91.2 2.5 %collective-permute-start.1 = (bf16[128,1536]{1,0:T(8,128)(2,1)}, bf16[128,1536]{1,0:T(8,128)(2,1)}, u32[]{:S(2)}, u32[]{:S(2)}) collective-permute-start(bf16[128,1536]{1,0:T(8,128)(2,1)} %get-tuple-element.27), channel_id=1, source_target_pairs={{0,2},{1,3},{2,0},{3,1},{4,6},{5,7},{6,4},{7,5},{8,10},{9,11},{10,... | collective-permute-start | bytes 1179656 | tf_op jit(solution)/shard_map/ppermute | solution.py:34
  93.7 1.4 collective-permute-start.2
  95.1 0.0 copy-start.3
  95.1 9.6 %copy.20 = f32[768,3072]{0,1:T(8,128)} copy(f32[768,3072]{1,0:T(8,128)} %param.16) | data formatting | bytes 18874368 | tf_op args[5]
  104.7 0.0 copy-done.3
  104.7 0.6 reduce_sum.68
  105.3 0.0 collective-permute-done
  105.3 14.8 %collective-permute-done.1 = bf16[128,1536]{1,0:T(8,128)(2,1)} collective-permute-done((bf16[128,1536]{1,0:T(8,128)(2,1)}, bf16[128,1536]{1,0:T(8,128)(2,1)}, u32[]{:S(2)}, u32[]{:S(2)}) %collective-permute-start.1) | collective-permute-done | bytes 393248 | tf_op jit(solution)/shard_map/ppermute | solution.py:34
  120.1 0.0 collective-permute-done.2
  120.1 2.2 add_convert_fusion
  122.3 1.7 copy.19
  124.0 0.0 all-to-all-done.1
  124.0 1.7 copy.22
  125.7 0.0 all-gather.3.cloned.1.call-done
  125.8 11.3 %fusion.5 = (f32[3072]{0:T(1024)S(1)}, f32[768]{0:T(1024)S(1)}, f32[3072,768]{1,0:T(8,128)}) fusion(bf16[1024,3072]{1,0:T(8,128)(2,1)} %all-gather.3.cloned.1.call-done, bf16[1024,768]{1,0:T(8,128)(2,1)S(1)} %bitcast.29), kind=kOutput, calls=%fused_computation.9 | convolution fusion | flops 4841271296 | bytes 17316864 | tf_op jit(solution)/shard_map/dot_general | solution.py:21
  137.0 17.9 %all-gather.5.cloned.1.call-done = bf16[1024,3072]{1,0:T(8,128)(2,1)} async-done(((bf16[128,3072]{1,0:T(8,128)(2,1)}), bf16[1024,3072]{1,0:T(8,128)(2,1)}) %all-gather.5.cloned.1.call-update) | async-done | bytes 6291472 | tf_op jit(solution)/shard_map/all_gather | solution.py:43
  155.0 0.0 copy-start.5
  155.0 0.0 copy-start.6
  155.0 11.3 %fusion.4 = (f32[3072]{0:T(1024)S(1)}, f32[768]{0:T(1024)S(1)}, f32[3072,768]{1,0:T(8,128)}) fusion(bf16[1024,3072]{1,0:T(8,128)(2,1)} %all-gather.5.cloned.1.call-done, bf16[1024,768]{1,0:T(8,128)(2,1)S(1)} %bitcast.28), kind=kOutput, calls=%fused_computation.8 | convolution fusion | flops 4841271296 | bytes 17316864 | tf_op jit(solution)/shard_map/dot_general | solution.py:21
  166.2 12.6 %all-reduce.1 = (f32[768]{0:T(1024)S(1)}, f32[768]{0:T(1024)S(1)}, f32[]{:T(128)}) all-reduce(f32[768]{0:T(1024)S(1)} %get-tuple-element.15, f32[768]{0:T(1024)S(1)} %get-tuple-element.13, f32[]{:T(128)} %reduce_sum.68), channel_id=1, replica_groups=mesh['dp'=8,'mp'=4] {'mp'}, use_global_device_ids=true, to_apply=%region_1.0 | all-reduce | flops 1537 | bytes 12296 | tf_op jit(solution)/shard_map/psum | solution.py:59
  178.8 0.0 copy-done.5
  178.8 0.0 copy-done.6
  178.8 0.7 multiply_add_fusion.3
  179.5 22.4 %all-reduce = (f32[]{:T(128)}, f32[3072]{0:T(1024)S(1)}, f32[]{:T(128)}, f32[3072]{0:T(1024)S(1)}) all-reduce(f32[]{:T(128)} %get-tuple-element.32, f32[3072]{0:T(1024)S(1)} %get-tuple-element.14, f32[]{:T(128)} %get-tuple-element.29, f32[3072]{0:T(1024)S(1)} %get-tuple-element.12), channel_id=1, replica_groups=mesh['dp'=8,'mp'=4] {'dp'}, use_global_device_ids=true, to_apply=%region_5.0 | all-reduce | flops 6146 | bytes 49168 | tf_op jit(solution)/shard_map/psum | solution.py:64
  201.9 0.0 copy-done.4
  202.6 11.2 %fusion.2 = f32[768,3072]{0,1:T(8,128)} fusion(f32[768,3072]{0,1:T(8,128)} %copy.20, f32[3072,768]{1,0:T(8,128)} %get-tuple-element.30, f32[]{:T(128)S(6)} %div.47, f32[3072]{0:T(1024)S(1)} %multiply_add_fusion.2, f32[768]{0:T(1024)S(1)} %get-tuple-element.33), kind=kLoop, calls=%fused_computation.4 | loop fusion | flops 11796480 | bytes 28326916 | tf_op jit(solution)/shard_map/sub | solution.py:79
  213.8 9.6 %copy.23 = f32[768,3072]{1,0:T(8,128)} copy(f32[768,3072]{0,1:T(8,128)} %fusion.2) | data formatting | bytes 18874368
  224.7 11.3 %multiply_subtract_fusion = f32[3072,768]{1,0:T(8,128)} fusion(f32[3072,768]{1,0:T(8,128)} %param.17, f32[3072,768]{1,0:T(8,128)} %get-tuple-element.31, f32[]{:T(128)S(6)} %div.54, f32[768]{0:T(1024)S(1)} %get-tuple-element.28, f32[3072]{0:T(1024)S(1)} %multiply_add_fusion.1), kind=kLoop, calls=%fused_computation.5 | loop fusion | flops 11796480 | bytes 28326916 | tf_op jit(solution)/shard_map/sub | solution.py:80
  (3 shorter events, 0.0 us)
Async XLA Ops:
  7.2 21.9 %copy-start.1 = (bf16[128,6144]{1,0:T(8,128)(2,1)S(1)}, bf16[128,6144]{1,0:T(8,128)(2,1)}, u32[]{:S(2)}) copy-start(bf16[128,6144]{1,0:T(8,128)(2,1)} %param.11) | copy-start | bytes 4718596
  7.2 118.6 %all-gather.3.cloned.1.call-start = ((), (), s32[]{:S(2)}) async-start(), calls=%async_computation.2 | async-start | bytes 7077888 | tf_op jit(solution)/shard_map/all_gather | solution.py:50
  26.4 9.4 %copy-start.2 = (bf16[128,6144]{1,0:T(8,128)(2,1)S(1)}, bf16[128,6144]{1,0:T(8,128)(2,1)}, u32[]{:S(2)}) copy-start(bf16[128,6144]{1,0:T(8,128)(2,1)} %param.13) | copy-start | bytes 4718596
  26.5 128.5 %all-gather.5.cloned.1.call-start = ((), (), s32[]{:S(2)}) async-start(), calls=%async_computation.3 | async-start | bytes 7077888 | tf_op jit(solution)/shard_map/all_gather | solution.py:43
  30.6 34.6 %all-to-all-start = ((bf16[128,8,768]{0,2,1:T(8,128)(2,1)}), bf16[128,8,768]{0,2,1:T(8,128)(2,1)S(1)}, u32[]{:S(2)}, u32[]{:S(2)}) async-start(bf16[128,8,768]{0,2,1:T(8,128)(2,1)} %bitcast), calls=%async_computation | async-start | bytes 3145728 | tf_op jit(solution)/shard_map/all_to_all | solution.py:45
  65.2 1.1 copy-start
  66.3 57.7 %all-to-all-start.1 = ((bf16[128,8,768]{0,2,1:T(8,128)(2,1)}), bf16[128,8,768]{0,2,1:T(8,128)(2,1)}, u32[]{:S(2)}, u32[]{:S(2)}) async-start(bf16[128,8,768]{0,2,1:T(8,128)(2,1)} %bitcast.4), calls=%async_computation.1 | async-start | bytes 3145728 | tf_op jit(solution)/shard_map/all_to_all | solution.py:44
  89.6 15.7 %collective-permute-start = (bf16[128,1536]{1,0:T(8,128)(2,1)}, bf16[128,1536]{1,0:T(8,128)(2,1)}, u32[]{:S(2)}, u32[]{:S(2)}) collective-permute-start(bf16[128,1536]{1,0:T(8,128)(2,1)} %get-tuple-element.25), channel_id=1, source_target_pairs={{0,1},{1,2},{2,3},{3,0},{4,5},{5,6},{6,7},{7,4},{8,9},{9,10},{10,1... | collective-permute-start | bytes 1179656 | tf_op jit(solution)/shard_map/ppermute | solution.py:34
  91.2 28.9 %collective-permute-start.1 = (bf16[128,1536]{1,0:T(8,128)(2,1)}, bf16[128,1536]{1,0:T(8,128)(2,1)}, u32[]{:S(2)}, u32[]{:S(2)}) collective-permute-start(bf16[128,1536]{1,0:T(8,128)(2,1)} %get-tuple-element.27), channel_id=1, source_target_pairs={{0,2},{1,3},{2,0},{3,1},{4,6},{5,7},{6,4},{7,5},{8,10},{9,11},{10,... | collective-permute-start | bytes 1179656 | tf_op jit(solution)/shard_map/ppermute | solution.py:34
  93.7 26.4 %collective-permute-start.2 = (bf16[128,1536]{1,0:T(8,128)(2,1)S(1)}, bf16[128,1536]{1,0:T(8,128)(2,1)}, u32[]{:S(2)}, u32[]{:S(2)}) collective-permute-start(bf16[128,1536]{1,0:T(8,128)(2,1)S(1)} %get-tuple-element.26), channel_id=1, source_target_pairs={{0,3},{1,0},{2,1},{3,2},{4,7},{5,4},{6,5},{7,6},{8,11},{9,8},{10,9... | collective-permute-start | bytes 1179656 | tf_op jit(solution)/shard_map/ppermute | solution.py:34
  95.1 9.6 %copy-start.3 = (f32[3072]{0:T(1024)S(1)}, f32[3072]{0:T(1024)}, u32[]{:S(2)}) copy-start(f32[3072]{0:T(1024)} %param.20) | copy-start | bytes 36868
  155.0 23.9 %copy-start.5 = (f32[768]{0:T(1024)S(1)}, f32[768]{0:T(1024)}, u32[]{:S(2)}) copy-start(f32[768]{0:T(1024)} %param.21) | copy-start | bytes 9220
  155.0 23.9 %copy-start.6 = (f32[768]{0:T(1024)S(1)}, f32[768]{0:T(1024)}, u32[]{:S(2)}) copy-start(f32[768]{0:T(1024)} %param.18) | copy-start | bytes 9220
  155.0 47.0 %copy-start.4 = (f32[3072]{0:T(1024)S(1)}, f32[3072]{0:T(1024)}, u32[]{:S(2)}) copy-start(f32[3072]{0:T(1024)} %param.19) | copy-start | bytes 36868
Sparse Core Ops, SparseCore 0:
  26.6 79.3 all-gather.2
  107.8 47.0 all-gather.4
where the time goes:
time: 243 us
  waiting for transfers between devices  60.5 us (25%)
  matrix products  59.7 us (25%)
  blocking collectives  35 us (14%)
  other arithmetic  28.4 us (12%)
  local copies, waits for them, and re-layouts  28 us (12%)
  between operations  16.1 us (7%)
  starting transfers between devices  15 us (6%)
    all_to_all x1, waiting for transfers between devices, body(): in_cols = lax.all_to_all(inputs, 'dp', 1, 0, tiled=True)  27.7 us
    unnamed x18, local copies, waits for them, and re-layouts  23.6 us
    dot_general x2, matrix products, contract_rows(): lax.dot_general(left, right, (((0,), (0,)), ((), ())), preferred_element_...  22.6 us
    psum x1, blocking collectives, body(): lax.psum((jnp.sum(square_in, axis=0), jnp.sum(square_out, axis=1), jnp.su...  22.4 us
    dot_general x1, matrix products, body(): lax.dot_general(out_grad, w_out, (((1,), (1,)), ((), ())), preferred_elem...  19.2 us
    dot_general x1, matrix products, body(): lax.dot_general(pre_grad, w_in, (((1,), (1,)), ((), ())), preferred_eleme...  18 us
    all_gather x1, waiting for transfers between devices, body(): lax.all_gather(active.astype(jnp.bfloat16), 'dp', axis=0, tiled=True)  17.9 us
    ppermute x3, waiting for transfers between devices, scatter_sum(): lax.ppermute(moved, axis, [(i, (i + shift) % size) for i in range(size)])  14.8 us
  transfers between devices with their start and end apart: 7, of which 3 were waited for; matrix products, arithmetic and copies ran while one was open for 21% of the time, Pallas kernels for 0%

commit v1 on v0

--- a/solution.py
+++ b/solution.py
@@ -42,7 +42,9 @@
     active, slope = gelu_parts(pre_act.astype(jnp.float32))
     hidden_all = lax.all_gather(active.astype(jnp.bfloat16), "dp", axis=0, tiled=True)
     out_cols = lax.all_to_all(out_grad, "dp", 1, 0, tiled=True)
-    in_cols = lax.all_to_all(inputs, "dp", 1, 0, tiled=True)
+    pieces = jnp.split(inputs, lax.axis_size("dp"), axis=1)
+    received = lax.all_to_all(jnp.stack(pieces), "dp", 0, 0)
+    in_cols = jnp.concatenate(received, axis=0)
     hid_grad = lax.dot_general(
         out_grad, w_out, (((1,), (1,)), ((), ())), preferred_element_type=jnp.float32
     )

time: 243 us -> 230 us (0.947)
  local copies, waits for them, and re-layouts: 28 us -> 14.2 us
  waiting for transfers between devices: 60.5 us -> 68.7 us
  other arithmetic: 28.4 us -> 21.8 us
    all_to_all x1, waiting for transfers between devices: 27.7 us -> 0.01 us  [body(): received = lax.all_to_all(jnp.stack(pieces), 'dp', 0, 0)]
    all_to_all x1, waiting for transfers between devices: 0.01 us -> 23.8 us  [body(): out_cols = lax.all_to_all(out_grad, 'dp', 1, 0, tiled=True)]
    unnamed x18 -> x36, local copies, waits for them, and re-layouts: 23.6 us -> 10.8 us
    ppermute x3, waiting for transfers between devices: 14.8 us -> 24.4 us  [scatter_sum(): lax.ppermute(moved, axis, [(i, (i + shift) % size) for i in range(size)])]
    sub x1, other arithmetic: 11.2 us -> 5.06 us  [body(): new_master_in = master_in - step_size * update_in]
    all_gather x1, waiting for transfers between devices: 17.9 us -> 20.4 us  [body(): lax.all_gather(active.astype(jnp.bfloat16), 'dp', axis=0, tiled=True)]
  transfers between devices with their start and end apart: 7 -> 7, of which waited for: 3 -> 4; matrix products, arithmetic and copies ran while one was open for 21% -> 18% of each run, Pallas kernels for 0% -> 0%
where the time goes in v1:
time: 230 us
  waiting for transfers between devices  68.7 us (30%)
  matrix products  58.9 us (26%)
  blocking collectives  35 us (15%)
  other arithmetic  21.8 us (9%)
  between operations  16.1 us (7%)
  starting transfers between devices  15.1 us (7%)
  local copies, waits for them, and re-layouts  14.2 us (6%)
    ppermute x3, waiting for transfers between devices, scatter_sum(): lax.ppermute(moved, axis, [(i, (i + shift) % size) for i in range(size)])  24.4 us
    all_to_all x1, waiting for transfers between devices, body(): out_cols = lax.all_to_all(out_grad, 'dp', 1, 0, tiled=True)  23.8 us
    psum x1, blocking collectives, body(): lax.psum((jnp.sum(square_in, axis=0), jnp.sum(square_out, axis=1), jnp.su...  22.4 us
    dot_general x2, matrix products, contract_rows(): lax.dot_general(left, right, (((0,), (0,)), ((), ())), preferred_element_...  21.8 us
    all_gather x1, waiting for transfers between devices, body(): lax.all_gather(active.astype(jnp.bfloat16), 'dp', axis=0, tiled=True)  20.4 us
    dot_general x1, matrix products, body(): lax.dot_general(out_grad, w_out, (((1,), (1,)), ((), ())), preferred_elem...  19.1 us
    dot_general x1, matrix products, body(): lax.dot_general(pre_grad, w_in, (((1,), (1,)), ((), ())), preferred_eleme...  17.9 us
    psum x1, blocking collectives, body(): lax.psum((jnp.sum(square_in, axis=1), jnp.sum(square_out, axis=0), jnp.su...  12.5 us
  transfers between devices with their start and end apart: 7, of which 4 were waited for; matrix products, arithmetic and copies ran while one was open for 18% of the time, Pallas kernels for 0%

profile of v1, /device:TPU:0, one launch (start us, length us, event | category | flops | bytes accessed | tf_op | source)
XLA Modules:
  0.0 229.9 jit_solution(6014334119231437913)
XLA Ops:
  7.2 0.0 all-gather.3.cloned.1.call-start
  7.2 19.1 %fusion.4 = bf16[128,3072]{1,0:T(8,128)(2,1)} fusion(bf16[128,6144]{1,0:T(8,128)(2,1)} %param.13, bf16[3072,6144]{1,0:T(8,128)(2,1)} %param.15, bf16[128,3072]{1,0:T(8,128)(2,1)} %param.12), kind=kOutput, calls=%fused_computation.9 | convolution fusion | flops 4836163584 | bytes 40894464 | tf_op jit(solution)/shard_map/dot_general | solution.py:48
  26.4 0.0 all-gather.3.cloned.1.call-update
  26.4 0.0 all-gather.5.cloned.1.call-start
  26.4 1.2 fusion.11
  27.7 0.0 all-gather.5.cloned.1.call-update
  27.7 0.2 copy-done.1
  27.9 1.6 copy.14
  29.4 5.3 %all-to-all-start.1 = ((bf16[128,8,768]{0,2,1:T(8,128)(2,1)}), bf16[128,8,768]{0,2,1:T(8,128)(2,1)S(1)}, u32[]{:S(2)}, u32[]{:S(2)}) async-start(bf16[128,8,768]{0,2,1:T(8,128)(2,1)} %bitcast.9), calls=%async_computation.1 | async-start | bytes 3145728 | tf_op jit(solution)/shard_map/all_to_all | solution.py:44
  34.8 0.7 bitcast_dynamic-update-slice_fusion.7
  35.5 0.7 bitcast_dynamic-update-slice_fusion.6
  36.1 0.7 bitcast_dynamic-update-slice_fusion.5
  36.8 0.7 bitcast_dynamic-update-slice_fusion.4
  37.5 0.7 bitcast_dynamic-update-slice_fusion.3
  38.2 0.7 bitcast_dynamic-update-slice_fusion.2
  38.9 0.7 bitcast_dynamic-update-slice_fusion.1
  39.6 0.7 bitcast_dynamic-update-slice_fusion
  40.3 23.8 %all-to-all-done.1 = bf16[128,8,768]{0,2,1:T(8,128)(2,1)S(1)} async-done(((bf16[128,8,768]{0,2,1:T(8,128)(2,1)}), bf16[128,8,768]{0,2,1:T(8,128)(2,1)S(1)}, u32[]{:S(2)}, u32[]{:S(2)}) %all-to-all-start.1) | async-done | bytes 1572896 | tf_op jit(solution)/shard_map/all_to_all | solution.py:44
  64.1 1.1 copy-done
  65.3 4.3 %all-to-all-start = ((bf16[8,128,768]{2,1,0:T(8,128)(2,1)}), bf16[8,128,768]{2,1,0:T(8,128)(2,1)}, u32[]{:S(2)}, u32[]{:S(2)}) async-start(bf16[8,128,768]{2,1,0:T(8,128)(2,1)} %bitcast_dynamic-update-slice_fusion), calls=%async_computation | async-start | bytes 3145728 | tf_op jit(solution)/shard_map/all_to_all | solution.py:46
  69.6 17.9 %fusion.13 = f32[128,6144]{1,0:T(8,128)S(1)} fusion(bf16[128,3072]{1,0:T(8,128)(2,1)} %fusion.4, bf16[6144,3072]{1,0:T(8,128)(2,1)} %param.14), kind=kOutput, calls=%fused_computation.39 | convolution fusion | flops 4831838208 | bytes 41680896 | tf_op jit(solution)/shard_map/dot_general | solution.py:53
  87.5 0.0 copy-start.4
  87.6 1.0 dynamic-slice_convert_fusion.2
  88.6 1.6 collective-permute-start
  90.2 2.5 %collective-permute-start.1 = (bf16[128,1536]{1,0:T(8,128)(2,1)}, bf16[128,1536]{1,0:T(8,128)(2,1)}, u32[]{:S(2)}, u32[]{:S(2)}) collective-permute-start(bf16[128,1536]{1,0:T(8,128)(2,1)} %get-tuple-element.18), channel_id=1, source_target_pairs={{0,2},{1,3},{2,0},{3,1},{4,6},{5,7},{6,4},{7,5},{8,10},{9,11},{10,... | collective-permute-start | bytes 1179656 | tf_op jit(solution)/shard_map/ppermute | solution.py:34
  92.7 1.4 collective-permute-start.2
  94.0 0.6 reduce_sum.68
  94.7 8.2 %collective-permute-done = bf16[128,1536]{1,0:T(8,128)(2,1)} collective-permute-done((bf16[128,1536]{1,0:T(8,128)(2,1)}, bf16[128,1536]{1,0:T(8,128)(2,1)}, u32[]{:S(2)}, u32[]{:S(2)}) %collective-permute-start) | collective-permute-done | bytes 393248 | tf_op jit(solution)/shard_map/ppermute | solution.py:34
  102.8 16.3 %collective-permute-done.1 = bf16[128,1536]{1,0:T(8,128)(2,1)} collective-permute-done((bf16[128,1536]{1,0:T(8,128)(2,1)}, bf16[128,1536]{1,0:T(8,128)(2,1)}, u32[]{:S(2)}, u32[]{:S(2)}) %collective-permute-start.1) | collective-permute-done | bytes 393248 | tf_op jit(solution)/shard_map/ppermute | solution.py:34
  119.1 0.0 collective-permute-done.2
  119.1 2.2 add_convert_fusion
  121.3 1.7 copy.15
  123.0 0.0 all-gather.3.cloned.1.call-done
  123.0 10.5 %fusion = (f32[3072]{0:T(1024)S(1)}, f32[768]{0:T(1024)S(1)}, f32[768,3072]{1,0:T(8,128)}) fusion(bf16[1024,768]{1,0:T(8,128)(2,1)} %bitcast.8, bf16[1024,3072]{1,0:T(8,128)(2,1)} %all-gather.3.cloned.1.call-done), kind=kOutput, calls=%fused_computation.4 | convolution fusion | flops 4841271296 | bytes 17316864 | tf_op jit(solution)/shard_map/dot_general | solution.py:21
  133.5 20.4 %all-gather.5.cloned.1.call-done = bf16[1024,3072]{1,0:T(8,128)(2,1)} async-done(((bf16[128,3072]{1,0:T(8,128)(2,1)}), bf16[1024,3072]{1,0:T(8,128)(2,1)}) %all-gather.5.cloned.1.call-update) | async-done | bytes 6291472 | tf_op jit(solution)/shard_map/all_gather | solution.py:43
  153.9 11.3 %fusion.3 = (f32[3072]{0:T(1024)S(1)}, f32[768]{0:T(1024)S(1)}, f32[3072,768]{1,0:T(8,128)}) fusion(bf16[1024,3072]{1,0:T(8,128)(2,1)} %all-gather.5.cloned.1.call-done, bf16[1024,768]{1,0:T(8,128)(2,1)S(1)} %bitcast.33), kind=kOutput, calls=%fused_computation.7 | convolution fusion | flops 4841271296 | bytes 17316864 | tf_op jit(solution)/shard_map/dot_general | solution.py:21
  165.2 12.5 %all-reduce.1 = (f32[768]{0:T(1024)S(1)}, f32[768]{0:T(1024)S(1)}, f32[]{:T(128)}) all-reduce(f32[768]{0:T(1024)S(1)} %get-tuple-element.6, f32[768]{0:T(1024)S(1)} %get-tuple-element.4, f32[]{:T(128)} %reduce_sum.68), channel_id=1, replica_groups=mesh['dp'=8,'mp'=4] {'mp'}, use_global_device_ids=true, to_apply=%region_1.0 | all-reduce | flops 1537 | bytes 12296 | tf_op jit(solution)/shard_map/psum | solution.py:61
  177.8 0.6 multiply_add_fusion.4
  178.4 22.4 %all-reduce = (f32[]{:T(128)}, f32[3072]{0:T(1024)S(1)}, f32[]{:T(128)}, f32[3072]{0:T(1024)S(1)}) all-reduce(f32[]{:T(128)} %get-tuple-element.23, f32[3072]{0:T(1024)S(1)} %get-tuple-element.5, f32[]{:T(128)} %get-tuple-element.20, f32[3072]{0:T(1024)S(1)} %get-tuple-element.3), channel_id=1, replica_groups=mesh['dp'=8,'mp'=4] {'dp'}, use_global_device_ids=true, to_apply=%region_5.0 | all-reduce | flops 6146 | bytes 49168 | tf_op jit(solution)/shard_map/psum | solution.py:66
  202.8 0.0 slice-start
  202.8 0.0 slice-start.3
  202.8 0.0 slice-start.4
  202.8 12.1 %multiply_subtract_fusion = f32[3072,768]{1,0:T(8,128)} fusion(f32[3072,768]{1,0:T(8,128)} %param.17, f32[3072,768]{1,0:T(8,128)} %get-tuple-element.22, f32[]{:T(128)S(6)} %div.54, f32[768]{0:T(1024)S(1)} %get-tuple-element.19, f32[3072]{0:T(1024)S(1)} %multiply_add_fusion.2), kind=kLoop, calls=%fused_computation | loop fusion | flops 11796480 | bytes 28326916 | tf_op jit(solution)/shard_map/sub | solution.py:82
  214.9 1.3 slice-done.1
  216.3 0.2 slice-done.2
  216.5 1.3 slice-done.4
  217.8 0.2 slice-done.5
  218.0 5.1 %multiply_subtract_fusion.1 = f32[768,3072]{1,0:T(8,128)} fusion(f32[768,3072]{1,0:T(8,128)S(1)} %bitcast.29, f32[768,3072]{1,0:T(8,128)S(1)} %bitcast.31, f32[]{:T(128)S(6)} %div.47, f32[3072]{0:T(1024)S(1)} %multiply_add_fusion.3, f32[768]{0:T(1024)S(1)} %get-tuple-element.24), kind=kLoop, calls=%fused_computation.2 | loop fusion | flops 11796480 | bytes 28326916 | tf_op jit(solution)/shard_map/sub | solution.py:81
  (23 shorter events, 0.1 us)
Async XLA Ops:
  7.2 19.3 %copy-start.3 = (bf16[128,3072]{1,0:T(8,128)(2,1)S(1)}, bf16[128,3072]{1,0:T(8,128)(2,1)}, u32[]{:S(2)}) copy-start(bf16[128,3072]{1,0:T(8,128)(2,1)} %param.12) | copy-start | bytes 2359300
  7.2 115.8 %all-gather.3.cloned.1.call-start = ((), (), s32[]{:S(2)}) async-start(), calls=%async_computation.2 | async-start | bytes 7077888 | tf_op jit(solution)/shard_map/all_gather | solution.py:52
  26.4 1.5 copy-start.1
  26.4 127.5 %all-gather.5.cloned.1.call-start = ((), (), s32[]{:S(2)}) async-start(), calls=%async_computation.3 | async-start | bytes 7077888 | tf_op jit(solution)/shard_map/all_gather | solution.py:43
  29.4 5.3 %copy-start.2 = (bf16[128,6144]{1,0:T(8,128)(2,1)S(1)}, bf16[128,6144]{1,0:T(8,128)(2,1)}, u32[]{:S(2)}) copy-start(bf16[128,6144]{1,0:T(8,128)(2,1)} %param.11) | copy-start | bytes 4718596
  29.4 34.7 %all-to-all-start.1 = ((bf16[128,8,768]{0,2,1:T(8,128)(2,1)}), bf16[128,8,768]{0,2,1:T(8,128)(2,1)S(1)}, u32[]{:S(2)}, u32[]{:S(2)}) async-start(bf16[128,8,768]{0,2,1:T(8,128)(2,1)} %bitcast.9), calls=%async_computation.1 | async-start | bytes 3145728 | tf_op jit(solution)/shard_map/all_to_all | solution.py:44
  64.1 1.1 copy-start
  65.3 57.7 %all-to-all-start = ((bf16[8,128,768]{2,1,0:T(8,128)(2,1)}), bf16[8,128,768]{2,1,0:T(8,128)(2,1)}, u32[]{:S(2)}, u32[]{:S(2)}) async-start(bf16[8,128,768]{2,1,0:T(8,128)(2,1)} %bitcast_dynamic-update-slice_fusion), calls=%async_computation | async-start | bytes 3145728 | tf_op jit(solution)/shard_map/all_to_all | solution.py:46
  87.5 6.5 %copy-start.4 = (f32[3072]{0:T(1024)S(1)}, f32[3072]{0:T(1024)}, u32[]{:S(2)}) copy-start(f32[3072]{0:T(1024)} %param.20) | copy-start | bytes 36868
  88.6 14.2 %collective-permute-start = (bf16[128,1536]{1,0:T(8,128)(2,1)}, bf16[128,1536]{1,0:T(8,128)(2,1)}, u32[]{:S(2)}, u32[]{:S(2)}) collective-permute-start(bf16[128,1536]{1,0:T(8,128)(2,1)} %get-tuple-element.16), channel_id=1, source_target_pairs={{0,1},{1,2},{2,3},{3,0},{4,5},{5,6},{6,7},{7,4},{8,9},{9,10},{10,1... | collective-permute-start | bytes 1179656 | tf_op jit(solution)/shard_map/ppermute | solution.py:34
  90.2 28.9 %collective-permute-start.1 = (bf16[128,1536]{1,0:T(8,128)(2,1)}, bf16[128,1536]{1,0:T(8,128)(2,1)}, u32[]{:S(2)}, u32[]{:S(2)}) collective-permute-start(bf16[128,1536]{1,0:T(8,128)(2,1)} %get-tuple-element.18), channel_id=1, source_target_pairs={{0,2},{1,3},{2,0},{3,1},{4,6},{5,7},{6,4},{7,5},{8,10},{9,11},{10,... | collective-permute-start | bytes 1179656 | tf_op jit(solution)/shard_map/ppermute | solution.py:34
  92.7 26.4 %collective-permute-start.2 = (bf16[128,1536]{1,0:T(8,128)(2,1)S(1)}, bf16[128,1536]{1,0:T(8,128)(2,1)}, u32[]{:S(2)}, u32[]{:S(2)}) collective-permute-start(bf16[128,1536]{1,0:T(8,128)(2,1)S(1)} %get-tuple-element.17), channel_id=1, source_target_pairs={{0,3},{1,0},{2,1},{3,2},{4,7},{5,4},{6,5},{7,6},{8,11},{9,8},{10,9... | collective-permute-start | bytes 1179656 | tf_op jit(solution)/shard_map/ppermute | solution.py:34
  153.9 23.9 %copy-start.6 = (f32[768]{0:T(1024)S(1)}, f32[768]{0:T(1024)}, u32[]{:S(2)}) copy-start(f32[768]{0:T(1024)} %param.21) | copy-start | bytes 9220
  153.9 23.9 %copy-start.7 = (f32[768]{0:T(1024)S(1)}, f32[768]{0:T(1024)}, u32[]{:S(2)}) copy-start(f32[768]{0:T(1024)} %param.18) | copy-start | bytes 9220
  153.9 48.2 %copy-start.5 = (f32[3072]{0:T(1024)S(1)}, f32[3072]{0:T(1024)}, u32[]{:S(2)}) copy-start(f32[3072]{0:T(1024)} %param.19) | copy-start | bytes 36868
  202.8 12.2 %slice-start = ((s8[9437184]{0:T(1024)(128)(4,1)}), s8[4194304]{0:T(1024)(128)(4,1)S(1)}, s32[]{:S(2)}) async-start(s8[9437184]{0:T(1024)(128)(4,1)} %bitcast.28), calls=%async_computation.4 | async-start | bytes 8388608
  202.8 12.2 %slice-start.3 = ((s8[9437184]{0:T(1024)(128)(4,1)}), s8[4194304]{0:T(1024)(128)(4,1)S(1)}, s32[]{:S(2)}) async-start(s8[9437184]{0:T(1024)(128)(4,1)} %bitcast.30), calls=%async_computation.7 | async-start | bytes 8388608
  202.8 13.5 %slice-start.1 = ((s8[9437184]{0:T(1024)(128)(4,1)}), s8[4194304]{0:T(1024)(128)(4,1)S(1)}, s32[]{:S(2)}) async-start(s8[9437184]{0:T(1024)(128)(4,1)} %bitcast.28), calls=%async_computation.5 | async-start | bytes 8388608
  202.8 13.7 %slice-start.2 = ((s8[9437184]{0:T(1024)(128)(4,1)}), s8[1048576]{0:T(1024)(128)(4,1)S(1)}, s32[]{:S(2)}) async-start(s8[9437184]{0:T(1024)(128)(4,1)} %bitcast.28), calls=%async_computation.6 | async-start | bytes 2097152
  202.8 15.0 %slice-start.4 = ((s8[9437184]{0:T(1024)(128)(4,1)}), s8[4194304]{0:T(1024)(128)(4,1)S(1)}, s32[]{:S(2)}) async-start(s8[9437184]{0:T(1024)(128)(4,1)} %bitcast.30), calls=%async_computation.8 | async-start | bytes 8388608
  202.8 15.2 %slice-start.5 = ((s8[9437184]{0:T(1024)(128)(4,1)}), s8[1048576]{0:T(1024)(128)(4,1)S(1)}, s32[]{:S(2)}) async-start(s8[9437184]{0:T(1024)(128)(4,1)} %bitcast.30), calls=%async_computation.9 | async-start | bytes 2097152
Sparse Core Ops, SparseCore 0:
  26.5 78.3 all-gather.2
  106.8 47.0 all-gather.4
